TPU v7x, 512 devices: a whole 4x4x16 slice. The times are simulated.
512 devices in a mesh: fsdp: 16 (over y, x), tp: 16 (over z), shift: 2 (over core).
Axes of the slice: x: 4, y: 4, z: 16, core: 2. Of those that a mesh axis runs over, the one named last changes fastest.
Arguments:
- w_query: float32 [10240, 5120], P(('shift', 'fsdp'), 'tp'), parts along dimension 0, may hold values from -0.125 to 0.125
- avg_query: float32 [10240, 5120], P(('shift', 'fsdp'), 'tp'), parts along dimension 0, may hold values from -0.078125 to 0.078125
- w_key: float32 [10240, 5120], P(('shift', 'fsdp'), 'tp'), parts along dimension 0, may hold values from -0.125 to 0.125
- avg_key: float32 [10240, 5120], P(('shift', 'fsdp'), 'tp'), parts along dimension 0, may hold values from -0.078125 to 0.078125
- w_value: float32 [10240, 5120], P(('shift', 'fsdp'), 'tp'), parts along dimension 0, may hold values from -0.125 to 0.125
- avg_value: float32 [10240, 5120], P(('shift', 'fsdp'), 'tp'), parts along dimension 0, may hold values from -0.078125 to 0.078125
- norm_train: float32 [10240], P(('shift', 'fsdp', 'tp')), parts along dimension 0, may hold values from 0.25 to 1.75
- norm_step: float32 [10240], P(('shift', 'fsdp', 'tp')), parts along dimension 0, may hold values from -0.3 to 0.3
Outputs:
- ready_query: bfloat16 [10240, 5120], P('shift', 'tp'), parts along dimension 0
- ready_key: bfloat16 [10240, 5120], P('shift', 'tp'), parts along dimension 0
- ready_value: bfloat16 [10240, 5120], P('shift', 'tp'), parts along dimension 0
- scale_query: float32 [10240], P(('shift', 'tp')), parts along dimension 0
- scale_key: float32 [10240], P(('shift', 'tp')), parts along dimension 0
- scale_value: float32 [10240], P(('shift', 'tp')), parts along dimension 0
- serve_norm: bfloat16 [10240], P('shift'), parts along dimension 0
- latest_query: float32 [10240, 5120], P(('shift', 'fsdp'), 'tp'), parts along dimension 0
- latest_key: float32 [10240, 5120], P(('shift', 'fsdp'), 'tp'), parts along dimension 0
- latest_value: float32 [10240, 5120], P(('shift', 'fsdp'), 'tp'), parts along dimension 0
There are 2 independent parts, one for each index of `shift`. A program takes and returns all parts, laid end to end along the dimension named above; each array names one. Nothing has to cross between parts.
All inputs are finite; a program needn't handle non-finite values. Where the computation divides by a largest or mean magnitude, that divisor is 1e-20 or more.
Results may differ from a plain program's by a relative error of at most 0.001.
Values may be sent and summed in bfloat16 or wider, within the bound.
No kernel may reach another device: no remote copies, remote signals or barrier semaphores. Data moves between devices by JAX's collectives and lax.ppermute only.
A program may use at most 128 MiB of HBM per device.

v0:
```python
import functools

import jax
import jax.numpy as jnp
from jax import lax
from jax.sharding import Mesh
from jax.sharding import PartitionSpec as P

D_MODEL = 5120
FSDP = ("fsdp_0", "fsdp_1")
FSDP_TP = ("fsdp_0", "fsdp_1", "tp")
SHIFT_FSDP = ("shift", "fsdp_0", "fsdp_1")
SHIFT_FSDP_TP = ("shift", "fsdp_0", "fsdp_1", "tp")


keep_rate = 0.7


def one_axis_at_a_time(value, axes):
    return functools.reduce(lax.psum, axes, value)


def in_one_piece(arrays, axis, dim, along):
    both = jnp.concatenate(arrays, axis=along)
    filled, at, gathered = (lax.all_gather(both, axis, axis=dim, tiled=True), 0, [])
    for a in arrays:
        gathered.append(lax.slice_in_dim(filled, at, at + a.shape[along], axis=along))
        at += a.shape[along]
    return tuple(gathered)


def laid_out(blocks, dim):
    blocks = jnp.moveaxis(blocks, 0, dim)
    dims = blocks.shape
    return blocks.reshape(*dims[:dim], dims[dim] * dims[dim + 1], *dims[dim + 2 :])


def all_blocks(value, axes, order):
    blocks = value
    for k in order:
        blocks = lax.all_gather(blocks, axes[k])
    done = order[::-1]
    back = [done.index(k) for k in range(len(axes))]
    blocks = blocks.transpose(*back, *range(len(axes), blocks.ndim))
    return blocks.reshape(-1, *value.shape)


def whole_of(value, axes, order, dim):
    return laid_out(all_blocks(value, axes, order), dim)


def shards(w_query, avg_query, w_key, avg_key, w_value, avg_value, norm_train, norm_step):
    latest_query = keep_rate * avg_query + (1.0 - keep_rate) * w_query
    latest_key = keep_rate * avg_key + (1.0 - keep_rate) * w_key
    latest_value = keep_rate * avg_value + (1.0 - keep_rate) * w_value
    total_query, total_key, total_value = (
        one_axis_at_a_time(jnp.sum(jnp.abs(latest_query), axis=0), FSDP),
        one_axis_at_a_time(jnp.sum(jnp.abs(latest_key), axis=0), FSDP),
        one_axis_at_a_time(jnp.sum(jnp.abs(latest_value), axis=0), FSDP),
    )
    scale_query = total_query / D_MODEL
    scale_key = total_key / D_MODEL
    scale_value = total_value / D_MODEL
    narrow_query, narrow_key, narrow_value = (
        (latest_query / scale_query).astype(jnp.bfloat16),
        (latest_key / scale_key).astype(jnp.bfloat16),
        (latest_value / scale_value).astype(jnp.bfloat16),
    )
    ready_query, ready_key, ready_value = in_one_piece(
        (narrow_query, narrow_key, narrow_value), FSDP, 0, 1
    )
    serve_norm = whole_of((norm_train + norm_step).astype(jnp.bfloat16), FSDP_TP, (0, 1, 2), 0)
    return (
        ready_query,
        ready_key,
        ready_value,
        scale_query,
        scale_key,
        scale_value,
        serve_norm,
        latest_query,
        latest_key,
        latest_value,
    )


def solution(mesh):
    split = Mesh(
        mesh.devices.reshape(4, 4, mesh.shape["tp"], mesh.shape["shift"]),
        ("fsdp_0", "fsdp_1", "tp", "shift"),
    )
    in_specs = (
        P(SHIFT_FSDP, "tp"),
        P(SHIFT_FSDP, "tp"),
        P(SHIFT_FSDP, "tp"),
        P(SHIFT_FSDP, "tp"),
        P(SHIFT_FSDP, "tp"),
        P(SHIFT_FSDP, "tp"),
        P(SHIFT_FSDP_TP),
        P(SHIFT_FSDP_TP),
    )
    out_specs = (
        P("shift", "tp"),
        P("shift", "tp"),
        P("shift", "tp"),
        P(("shift", "tp")),
        P(("shift", "tp")),
        P(("shift", "tp")),
        P("shift"),
        P(SHIFT_FSDP, "tp"),
        P(SHIFT_FSDP, "tp"),
        P(SHIFT_FSDP, "tp"),
    )
    return jax.shard_map(
        shards, mesh=split, in_specs=in_specs, out_specs=out_specs, check_vma=False
    )
```

profile of v0, /device:TPU:1, one launch (start us, length us, event | category | flops | bytes accessed | tf_op | source)
XLA Modules:
  0.0 162.6 jit_solution(14595157520068781043)
XLA Ops:
  7.2 0.0 all-gather.6.cloned.1.call-start
  7.2 1.3 abs_reduce_fusion.2
  8.6 1.9 %abs_reduce_fusion = (f32[320]{0:T(512)S(1)}, f32[320,320]{1,0:T(8,128)S(1)}, f32[320]{0:T(512)S(1)}, f32[320,320]{1,0:T(8,128)S(1)}) fusion(f32[320,320]{1,0:T(8,128)} %param.12, f32[320,320]{1,0:T(8,128)} %param.13, f32[320,320]{1,0:T(8,128)} %param.10, f32[320,320]{1,0:T(8,128)} %param.11), kind=kLoop, calls=%fused_computation.2 | loop fusion | flops 1023360 | bytes 2460160 | tf_op jit(solution)/shard_map/reduce_sum | solution.py:59
  10.4 0.0 copy-start.1
  10.4 0.0 copy-start.2
  10.5 9.6 %all-reduce.2 = (f32[320]{0:T(512)S(1)}, f32[320]{0:T(512)S(1)}, f32[320]{0:T(512)S(1)}) all-reduce(f32[320]{0:T(512)S(1)} %get-tuple-element.50, f32[320]{0:T(512)S(1)} %get-tuple-element.55, f32[320]{0:T(512)S(1)} %get-tuple-element.46), channel_id=1, replica_groups=mesh['fsdp_0'=4,'fsdp_1'=4,'tp'=16,'shift'=2] {'fsdp_0'}, use_global_device_ids=true, to_apply=%region_7.0 | all-reduce | flops 960 | bytes 7680 | tf_op jit(solution)/shard_map/psum | solution.py:20
  20.1 8.6 %all-reduce.1 = (f32[320]{0:T(512)S(1)}, f32[320]{0:T(512)S(1)}, f32[320]{0:T(512)S(1)}) all-reduce(f32[320]{0:T(512)S(1)} %get-tuple-element.43, f32[320]{0:T(512)S(1)} %get-tuple-element.44, f32[320]{0:T(512)S(1)} %get-tuple-element.45), channel_id=1, replica_groups=mesh['fsdp_0'=4,'fsdp_1'=4,'tp'=16,'shift'=2] {'fsdp_1'}, use_global_device_ids=true, to_apply=%region_8.0 | all-reduce | flops 960 | bytes 7680 | tf_op jit(solution)/shard_map/psum | solution.py:20
  28.7 0.0 copy-start.3
  28.7 0.0 copy-start.4
  28.7 0.0 copy-start.5
  28.9 1.0 pad_maximum_fusion
  29.9 0.0 all-gather.6.cloned.1.call-update
  29.9 1.3 dynamic-slice
  31.9 0.2 dynamic-update-slice
  32.1 6.0 %all-reduce = bf16[80]{0:T(256)(128)(2,1)S(1)} all-reduce(bf16[80]{0:T(256)(128)(2,1)S(1)} %dynamic-update-slice), channel_id=2, replica_groups=mesh['fsdp_0'=4,'fsdp_1'=4,'tp'=16,'shift'=2] {'fsdp_0'}, use_global_device_ids=true, to_apply=%add | all-reduce | flops 80 | bytes 320
  38.1 0.1 reshape.29
  38.2 5.2 %all-gather.3 = bf16[4,4,20]{2,1,0:T(4,128)(2,1)S(1)} all-gather(bf16[1,4,20]{2,1,0:T(4,128)(2,1)S(1)} %reshape.29), channel_id=3, replica_groups=mesh['fsdp_0'=4,'fsdp_1'=4,'tp'=16,'shift'=2] {'fsdp_1'}, dimensions={0}, use_global_device_ids=true | all-gather | bytes 800 | tf_op jit(solution)/shard_map/all_gather | solution.py:41
  43.4 30.7 %all-gather.2 = bf16[64,4,20]{2,1,0:T(4,128)(2,1)S(1)} all-gather(bf16[4,4,20]{2,1,0:T(4,128)(2,1)S(1)} %all-gather.3), channel_id=4, replica_groups=mesh['fsdp_0'=4,'fsdp_1'=4,'tp'=16,'shift'=2] {'tp'}, dimensions={0}, use_global_device_ids=true | all-gather | bytes 10880 | tf_op jit(solution)/shard_map/all_gather | solution.py:41
  74.2 0.7 reshape_reshape.3
  75.0 54.7 %all-gather.6.cloned.1.call-done = bf16[5120,960]{1,0:T(8,128)(2,1)} async-done(((bf16[320,960]{1,0:T(8,128)(2,1)}), bf16[5120,960]{1,0:T(8,128)(2,1)}) %all-gather.6.cloned.1.call-update) | async-done | bytes 9830416 | tf_op jit(solution)/shard_map/all_gather | solution.py:25
  129.6 8.4 %fusion = (bf16[5120,320]{1,0:T(8,128)(2,1)}, bf16[5120,320]{1,0:T(8,128)(2,1)}, bf16[5120,320]{1,0:T(8,128)(2,1)}) fusion(bf16[5120,960]{1,0:T(8,128)(2,1)} %all-gather.6.cloned.1.call-done), kind=kLoop, calls=%fused_computation.15 | loop fusion | bytes 19660800 | tf_op jit(solution)/shard_map/slice | solution.py:27
  138.1 5.9 %copy.26 = bf16[5120,320]{0,1:T(8,128)(2,1)} copy(bf16[5120,320]{1,0:T(8,128)(2,1)} %get-tuple-element.54) | data formatting | bytes 6553600
  144.0 5.9 %copy.27 = bf16[5120,320]{0,1:T(8,128)(2,1)} copy(bf16[5120,320]{1,0:T(8,128)(2,1)} %get-tuple-element.53) | data formatting | bytes 6553600
  149.9 5.9 %copy.28 = bf16[5120,320]{0,1:T(8,128)(2,1)} copy(bf16[5120,320]{1,0:T(8,128)(2,1)} %get-tuple-element.52) | data formatting | bytes 6553600
  (20 shorter events, 0.2 us)
Async XLA Ops:
  7.2 122.4 %all-gather.6.cloned.1.call-start = ((), (), s32[]{:S(2)}) async-start(), calls=%async_computation | async-start | bytes 11141120 | tf_op jit(solution)/shard_map/all_gather | solution.py:25
  8.5 129.5 %copy-start = (f32[320,320]{1,0:T(8,128)}, f32[320,320]{1,0:T(8,128)S(1)}, u32[]{:S(2)}) copy-start(f32[320,320]{1,0:T(8,128)S(1)} %get-tuple-element.47) | copy-start | bytes 1228804
  8.5 23.3 %copy-start.6 = (f32[20]{0:T(128)S(1)}, f32[20]{0:T(128)}, u32[]{:S(2)}) copy-start(f32[20]{0:T(128)} %param.14) | copy-start | bytes 244
  8.5 23.3 %copy-start.7 = (f32[20]{0:T(128)S(1)}, f32[20]{0:T(128)}, u32[]{:S(2)}) copy-start(f32[20]{0:T(128)} %param.15) | copy-start | bytes 244
  10.4 127.6 %copy-start.1 = (f32[320,320]{1,0:T(8,128)}, f32[320,320]{1,0:T(8,128)S(1)}, u32[]{:S(2)}) copy-start(f32[320,320]{1,0:T(8,128)S(1)} %get-tuple-element.51) | copy-start | bytes 1228804
  10.4 127.6 %copy-start.2 = (f32[320,320]{1,0:T(8,128)}, f32[320,320]{1,0:T(8,128)S(1)}, u32[]{:S(2)}) copy-start(f32[320,320]{1,0:T(8,128)S(1)} %get-tuple-element.56) | copy-start | bytes 1228804
  28.7 109.4 %copy-start.3 = (f32[320]{0:T(512)}, f32[320]{0:T(512)S(1)}, u32[]{:S(2)}) copy-start(f32[320]{0:T(512)S(1)} %broadcast_multiply_fusion.1) | copy-start | bytes 3844
  28.7 109.4 %copy-start.4 = (f32[320]{0:T(512)}, f32[320]{0:T(512)S(1)}, u32[]{:S(2)}) copy-start(f32[320]{0:T(512)S(1)} %broadcast_multiply_fusion) | copy-start | bytes 3844
  28.7 109.4 %copy-start.5 = (f32[320]{0:T(512)}, f32[320]{0:T(512)S(1)}, u32[]{:S(2)}) copy-start(f32[320]{0:T(512)S(1)} %broadcast_multiply_fusion.2) | copy-start | bytes 3844
Sparse Core Ops, SparseCore 0:
  30.0 99.5 all-gather.5
where the time goes:
time: 163 us
  blocking collectives  60.2 us (37%)
  waiting for transfers between devices  54.7 us (34%)
  local copies, waits for them, and re-layouts  28.5 us (17%)
  between operations  14.9 us (9%)
  other arithmetic  4.34 us (3%)
    all_gather x1, waiting for transfers between devices, in_one_piece(): lax.all_gather(both, axis, axis=dim, tiled=True)  54.7 us
    all_gather x2, blocking collectives, all_blocks(): blocks = lax.all_gather(blocks, axes[k])  36 us
    unnamed x23, local copies, waits for them, and re-layouts  19.3 us
    psum x2, blocking collectives, one_axis_at_a_time(): return functools.reduce(lax.psum, axes, value)  18.2 us
    slice x1, local copies, waits for them, and re-layouts, in_one_piece(): lax.slice_in_dim(filled, at, at + a.shape[along], axis=along)  8.44 us
    unnamed x1, blocking collectives  5.98 us
  transfers between devices with their start and end apart: 1, of which 1 were waited for; matrix products, arithmetic and copies ran while one was open for 1% of the time, Pallas kernels for 0%

commit v1 on v0

v1 whole, which is shorter than its diff:
```python
import functools

import jax
import jax.numpy as jnp
from jax import lax
from jax.experimental import pallas as pl
from jax.experimental.pallas import tpu as pltpu
from jax.sharding import Mesh
from jax.sharding import PartitionSpec as P


D_MODEL = 5120
FSDP = ("fsdp_0", "fsdp_1")
SHIFT_FSDP = ("shift", "fsdp_0", "fsdp_1")
SHIFT_FSDP_TP = ("shift", "fsdp_0", "fsdp_1", "tp")

keep_rate = 0.7

ROWS = 320
COLS = 320
NODES = 16
WIDTH = (256, 256, 224, 224)
START = (0, 256, 512, 736)
NEAR = ((0, 1), (1, 0), (2, 3), (3, 2))
FAR = ((1, 2), (2, 1), (3, 0), (0, 3))
CLASSES = (("fsdp_1", NEAR, 0), ("fsdp_1", FAR, 1), ("fsdp_0", NEAR, 0), ("fsdp_0", FAR, 1))
EARLY = (1, 2, 3)
ORDER = tuple(tuple((colour + step + 1) % 4 for step in range(4)) for colour in range(4))


def lines(colour):
    return WIDTH[colour] * 5 // 2


def average_kernel(wq, aq, wk, ak, wv, av, nt, ns, lq, lk, lv, sent, flat):
    flat[...] = jnp.zeros_like(flat)
    for m, (w, a, out) in enumerate(((wq, aq, lq), (wk, ak, lk), (wv, av, lv))):
        latest = keep_rate * a[...] + (1.0 - keep_rate) * w[...]
        out[...] = latest
        flat[m : m + 1, :COLS] = jnp.sum(jnp.abs(latest), axis=0, keepdims=True)
    flat[3:4, :20] = nt[...] + ns[...]
    row = lax.broadcasted_iota(jnp.int32, (8, 128), 0)
    lane = lax.broadcasted_iota(jnp.int32, (8, 128), 1)
    first, second, third = flat[:, :128], flat[:, 128:256], flat[:, 256:384]
    turned = pltpu.roll(third, 64, 1)
    packed = jnp.where(row < 4, first, pltpu.roll(second, 4, 0))
    packed = jnp.where((row == 3) & (lane >= 64), pltpu.roll(turned, 1, 0), packed)
    packed = jnp.where(
        row == 7,
        jnp.where(lane < 64, pltpu.roll(third, 7, 0), pltpu.roll(turned, 6, 0)),
        packed,
    )
    for node in range(NODES):
        sent[node] = packed


def pack_kernel(got, lq, lk, lv, m0, m1, m2, m3, sq, sk, sv, norm, wide):
    odd = lax.rem(lax.axis_index("fsdp_1"), 2) == 1
    total = got[0]
    for node in range(1, NODES):
        total = total + got[node]
    scale = total / D_MODEL
    turned = pltpu.roll(scale, 64, 1)
    tails = (scale[7:8], turned[7:8], turned[3:4])
    for m, (latest, out) in enumerate(((lq, sq), (lk, sk), (lv, sv))):
        parts = (scale[m : m + 1], scale[4 + m : 5 + m], tails[m][:, :64])
        for k, part in enumerate(parts):
            here = slice(128 * k, 128 * k + part.shape[1])
            out[here] = part[0]
            ready = latest[:, here] / part
            wide[COLS * m + here.start : COLS * m + here.stop, :ROWS] = ready.T
    norm[...] = jnp.zeros_like(norm)
    for node in range(NODES):
        norm[node : node + 1, :] = got[node, 3:4, :].astype(jnp.bfloat16)
    low = lax.broadcasted_iota(jnp.int32, (128, 128), 1) < 64
    for colour, out in enumerate((m0, m1, m2, m3)):
        width, start = WIDTH[colour], START[colour]
        half = width // 2
        mine = slice(start, start + width)

        @pl.when(jnp.logical_not(odd))
        def _(out=out, mine=mine, width=width, half=half):
            out[:width] = wide[mine, :128].astype(jnp.bfloat16)
            out[width : 2 * width] = wide[mine, 128:256].astype(jnp.bfloat16)
            rest = wide[mine, 256:384]
            both = jnp.where(low[:half], rest[:half], pltpu.roll(rest[half:], 64, 1))
            out[2 * width :] = both.astype(jnp.bfloat16)

        @pl.when(odd)
        def _(out=out, mine=mine, width=width, half=half):
            one = pltpu.roll(wide[mine, :128], 64, 1)
            two = pltpu.roll(wide[mine, 128:256], 64, 1)
            three = pltpu.roll(wide[mine, 256:384], 64, 1)
            cut = lax.broadcasted_iota(jnp.int32, (width, 128), 1) < 64
            out[:width] = jnp.where(cut, one, two).astype(jnp.bfloat16)
            out[width : 2 * width] = jnp.where(cut, two, three).astype(jnp.bfloat16)
            both = jnp.where(low[:half], pltpu.roll(one[half:], 64, 1), one[:half])
            out[2 * width :] = both.astype(jnp.bfloat16)


def place_of(colour, j):
    flips = {"fsdp_0": 0, "fsdp_1": 0}
    for step, cls in enumerate(ORDER[colour]):
        axis, _, bit = CLASSES[cls]
        if j >> step & 1:
            flips[axis] |= 1 << bit
    at = []
    for axis in FSDP:
        i = lax.axis_index(axis)
        gray = (i ^ (i >> 1)) ^ flips[axis]
        at.append(gray ^ (gray >> 1))
    return at[0] * 4 + at[1]


SEGMENTS = []
for _colour in range(4):
    _cut = []
    for _m in range(3):
        _lo = max(START[_colour], COLS * _m)
        _hi = min(START[_colour] + WIDTH[_colour], COLS * (_m + 1))
        if _lo < _hi:
            _cut.append((_m, _lo - COLS * _m, _lo - START[_colour], _hi - _lo))
    SEGMENTS.append(tuple(_cut))


def unpack_kernel(jobs, touched, given, *refs):
    outs = dict(zip(touched, refs[given : given + len(touched)]))
    scratch = refs[given + len(touched) :]
    started = []
    for n, (colour, pairs, halves) in enumerate(jobs):
        block, in_sem = scratch[4 * n], scratch[4 * n + 2]
        size = lines(colour)
        places = []
        for i, pair in enumerate(pairs):
            for j in pair:
                place = place_of(colour, j)
                slot = 2 * i + (place & 1)
                src = refs[halves[j // 8]].at[pl.ds((j % 8) * size, size)]
                pltpu.make_async_copy(src, block.at[slot], in_sem.at[slot]).start()
            places.append(place >> 1)
        started.append(places)
    going = []
    for n, (colour, _, halves) in enumerate(jobs):
        block, out, in_sem, out_sem = scratch[4 * n : 4 * n + 4]
        size, width = lines(colour), WIDTH[colour]
        half = width // 2
        low = lax.broadcasted_iota(jnp.int32, (half, 128), 1) < 64
        for i, place in enumerate(started[n]):
            for slot in (2 * i, 2 * i + 1):
                src = refs[min(halves.values())].at[pl.ds(0, size)]
                pltpu.make_async_copy(src, block.at[slot], in_sem.at[slot]).wait()
            even, odd = block.at[2 * i], block.at[2 * i + 1]
            lane = 640 * i
            out[:, lane : lane + 128] = even[:width]
            out[:, lane + 128 : lane + 256] = even[width : 2 * width]
            out[:, lane + 384 : lane + 512] = odd[:width]
            out[:, lane + 512 : lane + 640] = odd[width : 2 * width]
            e = even[2 * width :].astype(jnp.float32)
            o = odd[2 * width :].astype(jnp.float32)
            out[:half, lane + 256 : lane + 384] = jnp.where(low, e, o).astype(jnp.bfloat16)
            out[half:, lane + 256 : lane + 384] = pltpu.roll(
                jnp.where(low, o, e), 64, 1
            ).astype(jnp.bfloat16)
            there = pl.ds(pl.multiple_of(place * 640, 128), 640)
            for k, (m, to, at, many) in enumerate(SEGMENTS[colour]):
                copy = pltpu.make_async_copy(
                    out.at[pl.ds(at, many), pl.ds(lane, 640)],
                    outs[m].at[pl.ds(to, many), there],
                    out_sem.at[k, i],
                )
                copy.start()
                going.append(copy)
    for copy in going:
        copy.wait()


def unpacked(work, ready):
    values, jobs, scratch, size = [], [], [], 0
    for colour, nodes, halves in work:
        pairs = pairs_of(colour, nodes)
        at = {}
        for half, value in halves.items():
            at[half] = len(values)
            values.append(value)
        jobs.append((colour, pairs, at))
        scratch += [
            pltpu.VMEM((2 * len(pairs), lines(colour), 128), BF16),
            pltpu.VMEM((WIDTH[colour], 640 * len(pairs)), BF16),
            pltpu.SemaphoreType.DMA((2 * len(pairs),)),
            pltpu.SemaphoreType.DMA((2, len(pairs))),
        ]
        size += 4 * lines(colour) * 128 * len(pairs)
    touched = sorted({m for colour, _, _ in work for m, _, _, _ in SEGMENTS[colour]})
    begun = [m for m in touched if m in ready]
    given = len(values) + len(begun)
    result = pl.pallas_call(
        functools.partial(unpack_kernel, jobs, touched, given),
        out_shape=tuple(jax.ShapeDtypeStruct((COLS, D_MODEL), BF16) for _ in touched),
        in_specs=[ANY] * given,
        out_specs=[ANY] * len(touched),
        input_output_aliases={len(values) + i: touched.index(m) for i, m in enumerate(begun)},
        scratch_shapes=scratch,
        cost_estimate=pl.CostEstimate(flops=size, bytes_accessed=4 * size, transcendentals=0),
    )(*values, *(ready[m] for m in begun))
    ready.update(zip(touched, result))


def pairs_of(colour, nodes):
    flip = 1 << ORDER[colour].index(0)
    return tuple((j, j | flip) for j in nodes if not j & flip and j | flip in nodes)


VMEM = pl.BlockSpec(memory_space=pltpu.VMEM)
ANY = pl.BlockSpec(memory_space=pl.ANY)
F32 = jnp.float32
BF16 = jnp.bfloat16


def shards(w_query, avg_query, w_key, avg_key, w_value, avg_value, norm_train, norm_step):
    square = jax.ShapeDtypeStruct((ROWS, COLS), F32)
    lq, lk, lv, sums = pl.pallas_call(
        average_kernel,
        out_shape=(square,) * 3 + (jax.ShapeDtypeStruct((NODES, 8, 128), F32),),
        in_specs=[VMEM] * 8,
        out_specs=[VMEM] * 4,
        scratch_shapes=[pltpu.VMEM((8, 384), F32)],
    )(
        w_query,
        avg_query,
        w_key,
        avg_key,
        w_value,
        avg_value,
        norm_train.reshape(1, 20),
        norm_step.reshape(1, 20),
    )
    got = lax.all_to_all(sums, FSDP, 0, 0)
    row = jax.ShapeDtypeStruct((COLS,), F32)
    *own, sq, sk, sv, norm = pl.pallas_call(
        pack_kernel,
        out_shape=tuple(pltpu.VMEM((lines(c), 128), BF16) for c in range(4))
        + (row,) * 3
        + (jax.ShapeDtypeStruct((NODES, 128), BF16),),
        in_specs=[VMEM] * 4,
        out_specs=[VMEM] * 8,
        scratch_shapes=[pltpu.VMEM((3 * COLS, 384), F32)],
    )(got, lq, lk, lv)

    def exchanged(value, colour, step):
        axis, pairs, _ = CLASSES[ORDER[colour][step]]
        return lax.ppermute(value, axis, pairs)

    held = list(own)
    ready = {}
    for step in range(4):
        came = [exchanged(held[c], c, step) for c in range(4)]
        if step < 3:
            for c in range(4):
                both = jnp.concatenate([held[c], came[c]], axis=0)
                held[c] = lax.optimization_barrier(both)
    wide = jnp.broadcast_to(norm[None], (NODES, NODES, 128))
    norms = lax.all_to_all(wide, "tp", 0, 0)
    unpacked([(c, range(8), {0: held[c]}) for c in EARLY], ready)
    for c in range(4):
        if c in EARLY:
            unpacked([(c, range(8, 16), {1: came[c]})], ready)
        else:
            unpacked([(c, range(16), {0: held[c], 1: came[c]})], ready)
    serve_norm = norms[:, :, :20].transpose(1, 0, 2).reshape(D_MODEL)

    return (
        *(ready[m].T for m in range(3)),
        sq,
        sk,
        sv,
        serve_norm,
        lq,
        lk,
        lv,
    )


def solution(mesh):
    split = Mesh(
        mesh.devices.reshape(4, 4, mesh.shape["tp"], mesh.shape["shift"]),
        ("fsdp_0", "fsdp_1", "tp", "shift"),
    )
    in_specs = (P(SHIFT_FSDP, "tp"),) * 6 + (P(SHIFT_FSDP_TP),) * 2
    out_specs = (
        (P("shift", "tp"),) * 3
        + (P(("shift", "tp")),) * 3
        + (P("shift"),)
        + (P(SHIFT_FSDP, "tp"),) * 3
    )
    return jax.shard_map(
        shards, mesh=split, in_specs=in_specs, out_specs=out_specs, check_vma=False
    )
```

time: 163 us -> 124 us (0.76)
  the two profiles are of different devices: /device:TPU:1 before, /device:TPU:6 now
where the time goes in v1:
time: 124 us; the launch traced here: 123 us
  starting transfers between devices  49.7 us (40%)
  blocking collectives  43.1 us (35%)
  Pallas kernels  20 us (16%)
  waiting for transfers between devices  6.14 us (5%)
  other arithmetic  2.73 us (2%)
    ppermute x16, starting transfers between devices, exchanged(): return lax.ppermute(value, axis, pairs)  49.7 us
    all_to_all x1, blocking collectives, shards(): norms = lax.all_to_all(wide, 'tp', 0, 0)  27.6 us
    all_to_all x1, blocking collectives, shards(): got = lax.all_to_all(sums, FSDP, 0, 0)  15.5 us
    pallas_call x5, Pallas kernels, unpacked(): pl.pallas_call(functools.partial(unpack_kernel, jobs, touched, given), ou...  13.8 us
    ppermute x16, waiting for transfers between devices, exchanged(): return lax.ppermute(value, axis, pairs)  6.14 us
    pallas_call x1, Pallas kernels, shards(): pl.pallas_call(pack_kernel, out_shape=tuple((pltpu.VMEM((lines(c), 128),...  3.12 us
    pallas_call x1, Pallas kernels, shards(): pl.pallas_call(average_kernel, out_shape=(square,) * 3 + (jax.ShapeDtypeS...  3.01 us
    concatenate x12, other arithmetic, shards(): both = jnp.concatenate([held[c], came[c]], axis=0)  2.73 us
  transfers between devices with their start and end apart: 16, of which 2 were waited for; matrix products, arithmetic and copies ran while one was open for 3% of the time, Pallas kernels for 9%

profile of v1, /device:TPU:6, one launch (start us, length us, event | category | flops | bytes accessed | tf_op | source)
XLA Modules:
  0.0 123.4 jit_solution(7732958213030462949)
XLA Ops:
  0.6 3.0 %shard_map.159 = (f32[320,320]{1,0:T(8,128)}, f32[320,320]{1,0:T(8,128)}, f32[320,320]{1,0:T(8,128)}, f32[16,8,128]{2,1,0:T(8,128)}) custom-call(f32[320,320]{1,0:T(8,128)} %wq.1, f32[320,320]{1,0:T(8,128)} %aq.1, f32[320,320]{1,0:T(8,128)} %wk.1, f32[320,320]{1,0:T(8,128)} %ak.1, f32[320,320]{1,0:T(8,128)} %wv.1, f32[320,320]{1,0:T(8,128)} %av.1, ...), custom_call_target="tpu_custom_call" | custom-call | tf_op jit(solution)/shard_map/pallas_call | solution.py:221
  3.7 15.5 %all_to_all.10.got = f32[16,8,128]{2,1,0:T(8,128)} all-to-all(f32[16,8,128]{2,1,0:T(8,128)} %get-tuple-element.29), channel_id=1, replica_groups=mesh['fsdp_0'=4,'fsdp_1'=4,'tp'=16,'shift'=2] {'fsdp_0','fsdp_1'}, dimensions={0} | all-to-all | bytes 131072 | tf_op jit(solution)/shard_map/all_to_all | solution.py:237
  19.2 3.1 %shard_map.160 = (bf16[640,128]{1,0:T(8,128)(2,1)S(1)}, bf16[640,128]{1,0:T(8,128)(2,1)S(1)}, bf16[560,128]{1,0:T(8,128)(2,1)S(1)}, bf16[560,128]{1,0:T(8,128)(2...) custom-call(f32[16,8,128]{2,1,0:T(8,128)} %all_to_all.10.got, ...), custom_call_target="tpu_custom_call" | custom-call | tf_op jit(solution)/shard_map/pallas_call | solution.py:239
  24.6 3.0 %collective-permute-start.8 = (bf16[560,128]{1,0:T(8,128)(2,1)S(1)}, bf16[560,128]{1,0:T(8,128)(2,1)S(1)}, u32[]{:S(2)}, u32[]{:S(2)}) collective-permute-start(bf16[560,128]{1,0:T(8,128)(2,1)S(1)} %get-tuple-element.35), channel_id=1, source_target_pairs={{128,256},{256,128},{384,0},{0,384},{129,257},{257,129},{385,1},{1... | collective-permute-start | bytes 430088 | tf_op jit(solution)/shard_map/ppermute | solution.py:251
  29.6 4.2 %collective-permute-start.4 = (bf16[640,128]{1,0:T(8,128)(2,1)S(1)}, bf16[640,128]{1,0:T(8,128)(2,1)S(1)}, u32[]{:S(2)}, u32[]{:S(2)}) collective-permute-start(bf16[640,128]{1,0:T(8,128)(2,1)S(1)} %get-tuple-element.34), channel_id=1, source_target_pairs={{32,64},{64,32},{96,0},{0,96},{33,65},{65,33},{97,1},{1,97},{34,66... | collective-permute-start | bytes 491528 | tf_op jit(solution)/shard_map/ppermute | solution.py:251
  33.8 2.9 %collective-permute-start.12 = (bf16[1120,128]{1,0:T(8,128)(2,1)S(1)}, bf16[1120,128]{1,0:T(8,128)(2,1)S(1)}, u32[]{:S(2)}, u32[]{:S(2)}) collective-permute-start(bf16[1120,128]{1,0:T(8,128)(2,1)S(1)} %pad_maximum_fusion.11), channel_id=1, source_target_pairs={{32,64},{64,32},{96,0},{0,96},{33,65},{65,33},{97,1},{1,97},{34,66... | collective-permute-start | bytes 860168 | tf_op jit(solution)/shard_map/ppermute | solution.py:251
  36.8 2.4 %collective-permute-start.9 = (bf16[1120,128]{1,0:T(8,128)(2,1)S(1)}, bf16[1120,128]{1,0:T(8,128)(2,1)S(1)}, u32[]{:S(2)}, u32[]{:S(2)}) collective-permute-start(bf16[1120,128]{1,0:T(8,128)(2,1)S(1)} %pad_maximum_fusion.10), channel_id=1, source_target_pairs={{0,32},{32,0},{64,96},{96,64},{1,33},{33,1},{65,97},{97,65},{2,34}... | collective-permute-start | bytes 860168 | tf_op jit(solution)/shard_map/ppermute | solution.py:251
  39.2 4.0 %collective-permute-start.1 = (bf16[1280,128]{1,0:T(8,128)(2,1)S(1)}, bf16[1280,128]{1,0:T(8,128)(2,1)S(1)}, u32[]{:S(2)}, u32[]{:S(2)}) collective-permute-start(bf16[1280,128]{1,0:T(8,128)(2,1)S(1)} %pad_maximum_fusion.8), channel_id=1, source_target_pairs={{128,256},{256,128},{384,0},{0,384},{129,257},{257,129},{385,1},{1... | collective-permute-start | bytes 983048 | tf_op jit(solution)/shard_map/ppermute | solution.py:251
  43.2 3.3 %collective-permute-start.5 = (bf16[1280,128]{1,0:T(8,128)(2,1)S(1)}, bf16[1280,128]{1,0:T(8,128)(2,1)S(1)}, u32[]{:S(2)}, u32[]{:S(2)}) collective-permute-start(bf16[1280,128]{1,0:T(8,128)(2,1)S(1)} %pad_maximum_fusion.9), channel_id=1, source_target_pairs={{0,128},{128,0},{256,384},{384,256},{1,129},{129,1},{257,385},{385... | collective-permute-start | bytes 983048 | tf_op jit(solution)/shard_map/ppermute | solution.py:251
  46.6 2.5 %collective-permute-start.13 = (bf16[2240,128]{1,0:T(8,128)(2,1)S(1)}, bf16[2240,128]{1,0:T(8,128)(2,1)S(1)}, u32[]{:S(2)}, u32[]{:S(2)}) collective-permute-start(bf16[2240,128]{1,0:T(8,128)(2,1)S(1)} %pad_maximum_fusion.7), channel_id=1, source_target_pairs={{0,128},{128,0},{256,384},{384,256},{1,129},{129,1},{257,385},{385... | collective-permute-start | bytes 1720328 | tf_op jit(solution)/shard_map/ppermute | solution.py:251
  49.2 3.8 %collective-permute-start.10 = (bf16[2240,128]{1,0:T(8,128)(2,1)S(1)}, bf16[2240,128]{1,0:T(8,128)(2,1)S(1)}, u32[]{:S(2)}, u32[]{:S(2)}) collective-permute-start(bf16[2240,128]{1,0:T(8,128)(2,1)S(1)} %pad_maximum_fusion.6), channel_id=1, source_target_pairs={{32,64},{64,32},{96,0},{0,96},{33,65},{65,33},{97,1},{1,97},{34,66... | collective-permute-start | bytes 1720328 | tf_op jit(solution)/shard_map/ppermute | solution.py:251
  53.0 3.3 %collective-permute-start.2 = (bf16[2560,128]{1,0:T(8,128)(2,1)S(1)}, bf16[2560,128]{1,0:T(8,128)(2,1)S(1)}, u32[]{:S(2)}, u32[]{:S(2)}) collective-permute-start(bf16[2560,128]{1,0:T(8,128)(2,1)S(1)} %pad_maximum_fusion.4), channel_id=1, source_target_pairs={{0,32},{32,0},{64,96},{96,64},{1,33},{33,1},{65,97},{97,65},{2,34}... | collective-permute-start | bytes 1966088 | tf_op jit(solution)/shard_map/ppermute | solution.py:251
  56.4 3.1 %collective-permute-start.6 = (bf16[2560,128]{1,0:T(8,128)(2,1)S(1)}, bf16[2560,128]{1,0:T(8,128)(2,1)S(1)}, u32[]{:S(2)}, u32[]{:S(2)}) collective-permute-start(bf16[2560,128]{1,0:T(8,128)(2,1)S(1)} %pad_maximum_fusion.5), channel_id=1, source_target_pairs={{128,256},{256,128},{384,0},{0,384},{129,257},{257,129},{385,1},{1... | collective-permute-start | bytes 1966088 | tf_op jit(solution)/shard_map/ppermute | solution.py:251
  59.4 2.5 %collective-permute-done.10 = bf16[2240,128]{1,0:T(8,128)(2,1)S(1)} collective-permute-done((bf16[2240,128]{1,0:T(8,128)(2,1)S(1)}, bf16[2240,128]{1,0:T(8,128)(2,1)S(1)}, u32[]{:S(2)}, u32[]{:S(2)}) %collective-permute-start.10) | collective-permute-done | bytes 573472 | tf_op jit(solution)/shard_map/ppermute | solution.py:251
  63.1 3.3 %collective-permute-start.14 = (bf16[4480,128]{1,0:T(8,128)(2,1)}, bf16[4480,128]{1,0:T(8,128)(2,1)}, u32[]{:S(2)}, u32[]{:S(2)}) collective-permute-start(bf16[4480,128]{1,0:T(8,128)(2,1)} %pad_maximum_fusion.2.refs_1_), channel_id=1, source_target_pairs={{0,128},{128,0},{256,384},{384,256},{1,129},{129,1},{257,385},{385... | collective-permute-start | bytes 3440648 | tf_op jit(solution)/shard_map/ppermute | solution.py:251
  66.5 3.6 %collective-permute-done.6 = bf16[2560,128]{1,0:T(8,128)(2,1)S(1)} collective-permute-done((bf16[2560,128]{1,0:T(8,128)(2,1)S(1)}, bf16[2560,128]{1,0:T(8,128)(2,1)S(1)}, u32[]{:S(2)}, u32[]{:S(2)}) %collective-permute-start.6) | collective-permute-done | bytes 655392 | tf_op jit(solution)/shard_map/ppermute | solution.py:251
  70.2 2.7 %collective-permute-start.7 = (bf16[5120,128]{1,0:T(8,128)(2,1)S(1)}, bf16[5120,128]{1,0:T(8,128)(2,1)}, u32[]{:S(2)}, u32[]{:S(2)}) collective-permute-start(bf16[5120,128]{1,0:T(8,128)(2,1)S(1)} %pad_maximum_fusion.1.refs_0_), channel_id=1, source_target_pairs={{0,32},{32,0},{64,96},{96,64},{1,33},{33,1},{65,97},{97,65},{2,34}... | collective-permute-start | bytes 3932168 | tf_op jit(solution)/shard_map/ppermute | solution.py:251
  72.8 4.1 %collective-permute-start.3 = (bf16[5120,128]{1,0:T(8,128)(2,1)S(1)}, bf16[5120,128]{1,0:T(8,128)(2,1)}, u32[]{:S(2)}, u32[]{:S(2)}) collective-permute-start(bf16[5120,128]{1,0:T(8,128)(2,1)S(1)} %pad_maximum_fusion.refs_0_), channel_id=1, source_target_pairs={{32,64},{64,32},{96,0},{0,96},{33,65},{65,33},{97,1},{1,97},{34,66... | collective-permute-start | bytes 3932168 | tf_op jit(solution)/shard_map/ppermute | solution.py:251
  78.1 3.0 %collective-permute-start.15 = (bf16[4480,128]{1,0:T(8,128)(2,1)}, bf16[4480,128]{1,0:T(8,128)(2,1)}, u32[]{:S(2)}, u32[]{:S(2)}) collective-permute-start(bf16[4480,128]{1,0:T(8,128)(2,1)} %pad_maximum_fusion.3.refs_2_), channel_id=1, source_target_pairs={{128,256},{256,128},{384,0},{0,384},{129,257},{257,129},{385,1},{1... | collective-permute-start | bytes 3440648 | tf_op jit(solution)/shard_map/ppermute | solution.py:251
  81.2 27.6 %all_to_all.11 = bf16[16,16,128]{2,1,0:T(8,128)(2,1)S(1)} all-to-all(bf16[16,16,128]{2,1,0:T(8,128)(2,1)S(1)} %broadcast_in_dim.2), channel_id=1, replica_groups=mesh['fsdp_0'=4,'fsdp_1'=4,'tp'=16,'shift'=2] {'tp'}, dimensions={0} | all-to-all | bytes 131072 | tf_op jit(solution)/shard_map/all_to_all | solution.py:262
  109.5 4.0 %shard_map.161 = (bf16[320,5120]{1,0:T(8,128)(2,1)}, bf16[320,5120]{1,0:T(8,128)(2,1)}, bf16[320,5120]{1,0:T(8,128)(2,1)}) custom-call(bf16[5120,128]{1,0:T(8,128)(2,1)} %copy-done, bf16[4480,128]{1,0:T(8,128)(2,1)} %pad_maximum_fusion.2.refs_1_, bf16[4480,128]{1,0:T(8,128)(2,1)} %pad_maximum_fusion.3.refs_2_), custom_call_target="tpu_custom_call" | custom-call | flops 3604480 | bytes 14417920 | tf_op jit(solution)/shard_map/pallas_call | solution.py:196
  113.5 2.9 %shard_map.162.refs_1_ = bf16[320,5120]{1,0:T(8,128)(2,1)} custom-call(bf16[5120,128]{1,0:T(8,128)(2,1)} %copy-done.1, bf16[5120,128]{1,0:T(8,128)(2,1)} %collective-permute-done.7.refs_1_, bf16[320,5120]{1,0:T(8,128)(2,1)} %get-tuple-element.37.refs_2_), custom_call_target="tpu_custom_call", output_to_operand_aliasing={{}: (2, {})} | custom-call | flops 2621440 | bytes 10485760 | tf_op jit(solution)/shard_map/pallas_call | solution.py:196
  116.5 2.4 %shard_map.163 = (bf16[320,5120]{1,0:T(8,128)(2,1)}, bf16[320,5120]{1,0:T(8,128)(2,1)}) custom-call(bf16[5120,128]{1,0:T(8,128)(2,1)} %collective-permute-done.3.refs_0_, bf16[320,5120]{1,0:T(8,128)(2,1)} %shard_map.162.refs_1_, bf16[320,5120]{1,0:T(8,128)(2,1)} %get-tuple-element.38.refs_2_), custom_call_target="tpu_custom_call", output_to_operand_aliasing={{0}: (1, {}), {1}: (2, {})} | custom-call | flops 1310720 | bytes 5242880 | tf_op jit(solution)/shard_map/pallas_call | solution.py:196
  121.1 2.3 %shard_map.165 = bf16[320,5120]{1,0:T(8,128)(2,1)} custom-call(bf16[4480,128]{1,0:T(8,128)(2,1)} %collective-permute-done.15.refs_0_, bf16[320,5120]{1,0:T(8,128)(2,1)} %get-tuple-element.43.refs_1_), custom_call_target="tpu_custom_call", output_to_operand_aliasing={{}: (1, {})} | custom-call | flops 1146880 | bytes 4587520 | tf_op jit(solution)/shard_map/pallas_call | solution.py:196
  (39 shorter events, 10.0 us)
Async XLA Ops:
  22.3 11.5 %collective-permute-start.11 = (bf16[560,128]{1,0:T(8,128)(2,1)S(1)}, bf16[560,128]{1,0:T(8,128)(2,1)S(1)}, u32[]{:S(2)}, u32[]{:S(2)}) collective-permute-start(bf16[560,128]{1,0:T(8,128)(2,1)S(1)} %get-tuple-element.36), channel_id=1, source_target_pairs={{0,32},{32,0},{64,96},{96,64},{1,33},{33,1},{65,97},{97,65},{2,34}... | collective-permute-start | bytes 430088 | tf_op jit(solution)/shard_map/ppermute | solution.py:251
  24.6 12.1 %collective-permute-start.8 = (bf16[560,128]{1,0:T(8,128)(2,1)S(1)}, bf16[560,128]{1,0:T(8,128)(2,1)S(1)}, u32[]{:S(2)}, u32[]{:S(2)}) collective-permute-start(bf16[560,128]{1,0:T(8,128)(2,1)S(1)} %get-tuple-element.35), channel_id=1, source_target_pairs={{128,256},{256,128},{384,0},{0,384},{129,257},{257,129},{385,1},{1... | collective-permute-start | bytes 430088 | tf_op jit(solution)/shard_map/ppermute | solution.py:251
  27.6 11.5 %collective-permute-start = (bf16[640,128]{1,0:T(8,128)(2,1)S(1)}, bf16[640,128]{1,0:T(8,128)(2,1)S(1)}, u32[]{:S(2)}, u32[]{:S(2)}) collective-permute-start(bf16[640,128]{1,0:T(8,128)(2,1)S(1)} %get-tuple-element.33), channel_id=1, source_target_pairs={{0,128},{128,0},{256,384},{384,256},{1,129},{129,1},{257,385},{385... | collective-permute-start | bytes 491528 | tf_op jit(solution)/shard_map/ppermute | solution.py:251
  29.6 13.5 %collective-permute-start.4 = (bf16[640,128]{1,0:T(8,128)(2,1)S(1)}, bf16[640,128]{1,0:T(8,128)(2,1)S(1)}, u32[]{:S(2)}, u32[]{:S(2)}) collective-permute-start(bf16[640,128]{1,0:T(8,128)(2,1)S(1)} %get-tuple-element.34), channel_id=1, source_target_pairs={{32,64},{64,32},{96,0},{0,96},{33,65},{65,33},{97,1},{1,97},{34,66... | collective-permute-start | bytes 491528 | tf_op jit(solution)/shard_map/ppermute | solution.py:251
  33.8 12.7 %collective-permute-start.12 = (bf16[1120,128]{1,0:T(8,128)(2,1)S(1)}, bf16[1120,128]{1,0:T(8,128)(2,1)S(1)}, u32[]{:S(2)}, u32[]{:S(2)}) collective-permute-start(bf16[1120,128]{1,0:T(8,128)(2,1)S(1)} %pad_maximum_fusion.11), channel_id=1, source_target_pairs={{32,64},{64,32},{96,0},{0,96},{33,65},{65,33},{97,1},{1,97},{34,66... | collective-permute-start | bytes 860168 | tf_op jit(solution)/shard_map/ppermute | solution.py:251
  36.8 12.3 %collective-permute-start.9 = (bf16[1120,128]{1,0:T(8,128)(2,1)S(1)}, bf16[1120,128]{1,0:T(8,128)(2,1)S(1)}, u32[]{:S(2)}, u32[]{:S(2)}) collective-permute-start(bf16[1120,128]{1,0:T(8,128)(2,1)S(1)} %pad_maximum_fusion.10), channel_id=1, source_target_pairs={{0,32},{32,0},{64,96},{96,64},{1,33},{33,1},{65,97},{97,65},{2,34}... | collective-permute-start | bytes 860168 | tf_op jit(solution)/shard_map/ppermute | solution.py:251
  39.2 13.7 %collective-permute-start.1 = (bf16[1280,128]{1,0:T(8,128)(2,1)S(1)}, bf16[1280,128]{1,0:T(8,128)(2,1)S(1)}, u32[]{:S(2)}, u32[]{:S(2)}) collective-permute-start(bf16[1280,128]{1,0:T(8,128)(2,1)S(1)} %pad_maximum_fusion.8), channel_id=1, source_target_pairs={{128,256},{256,128},{384,0},{0,384},{129,257},{257,129},{385,1},{1... | collective-permute-start | bytes 983048 | tf_op jit(solution)/shard_map/ppermute | solution.py:251
  43.2 13.1 %collective-permute-start.5 = (bf16[1280,128]{1,0:T(8,128)(2,1)S(1)}, bf16[1280,128]{1,0:T(8,128)(2,1)S(1)}, u32[]{:S(2)}, u32[]{:S(2)}) collective-permute-start(bf16[1280,128]{1,0:T(8,128)(2,1)S(1)} %pad_maximum_fusion.9), channel_id=1, source_target_pairs={{0,128},{128,0},{256,384},{384,256},{1,129},{129,1},{257,385},{385... | collective-permute-start | bytes 983048 | tf_op jit(solution)/shard_map/ppermute | solution.py:251
  46.6 30.4 %collective-permute-start.13 = (bf16[2240,128]{1,0:T(8,128)(2,1)S(1)}, bf16[2240,128]{1,0:T(8,128)(2,1)S(1)}, u32[]{:S(2)}, u32[]{:S(2)}) collective-permute-start(bf16[2240,128]{1,0:T(8,128)(2,1)S(1)} %pad_maximum_fusion.7), channel_id=1, source_target_pairs={{0,128},{128,0},{256,384},{384,256},{1,129},{129,1},{257,385},{385... | collective-permute-start | bytes 1720328 | tf_op jit(solution)/shard_map/ppermute | solution.py:251
  49.2 12.8 %collective-permute-start.10 = (bf16[2240,128]{1,0:T(8,128)(2,1)S(1)}, bf16[2240,128]{1,0:T(8,128)(2,1)S(1)}, u32[]{:S(2)}, u32[]{:S(2)}) collective-permute-start(bf16[2240,128]{1,0:T(8,128)(2,1)S(1)} %pad_maximum_fusion.6), channel_id=1, source_target_pairs={{32,64},{64,32},{96,0},{0,96},{33,65},{65,33},{97,1},{1,97},{34,66... | collective-permute-start | bytes 1720328 | tf_op jit(solution)/shard_map/ppermute | solution.py:251
  53.0 13.4 %collective-permute-start.2 = (bf16[2560,128]{1,0:T(8,128)(2,1)S(1)}, bf16[2560,128]{1,0:T(8,128)(2,1)S(1)}, u32[]{:S(2)}, u32[]{:S(2)}) collective-permute-start(bf16[2560,128]{1,0:T(8,128)(2,1)S(1)} %pad_maximum_fusion.4), channel_id=1, source_target_pairs={{0,32},{32,0},{64,96},{96,64},{1,33},{33,1},{65,97},{97,65},{2,34}... | collective-permute-start | bytes 1966088 | tf_op jit(solution)/shard_map/ppermute | solution.py:251
  56.4 13.7 %collective-permute-start.6 = (bf16[2560,128]{1,0:T(8,128)(2,1)S(1)}, bf16[2560,128]{1,0:T(8,128)(2,1)S(1)}, u32[]{:S(2)}, u32[]{:S(2)}) collective-permute-start(bf16[2560,128]{1,0:T(8,128)(2,1)S(1)} %pad_maximum_fusion.5), channel_id=1, source_target_pairs={{128,256},{256,128},{384,0},{0,384},{129,257},{257,129},{385,1},{1... | collective-permute-start | bytes 1966088 | tf_op jit(solution)/shard_map/ppermute | solution.py:251
  63.1 55.8 %collective-permute-start.14 = (bf16[4480,128]{1,0:T(8,128)(2,1)}, bf16[4480,128]{1,0:T(8,128)(2,1)}, u32[]{:S(2)}, u32[]{:S(2)}) collective-permute-start(bf16[4480,128]{1,0:T(8,128)(2,1)} %pad_maximum_fusion.2.refs_1_), channel_id=1, source_target_pairs={{0,128},{128,0},{256,384},{384,256},{1,129},{129,1},{257,385},{385... | collective-permute-start | bytes 3440648 | tf_op jit(solution)/shard_map/ppermute | solution.py:251
  66.5 6.3 %copy-start = (bf16[5120,128]{1,0:T(8,128)(2,1)}, bf16[5120,128]{1,0:T(8,128)(2,1)S(1)}, u32[]{:S(2)}) copy-start(bf16[5120,128]{1,0:T(8,128)(2,1)S(1)} %pad_maximum_fusion.refs_0_) | copy-start | bytes 3932164
  70.1 38.6 %copy-start.1 = (bf16[5120,128]{1,0:T(8,128)(2,1)}, bf16[5120,128]{1,0:T(8,128)(2,1)S(1)}, u32[]{:S(2)}) copy-start(bf16[5120,128]{1,0:T(8,128)(2,1)S(1)} %pad_maximum_fusion.1.refs_0_) | copy-start | bytes 3932164
  70.1 11.0 %copy-start.2 = (bf16[16,128]{1,0:T(8,128)(2,1)S(1)}, bf16[16,128]{1,0:T(8,128)(2,1)}, u32[]{:S(2)}) copy-start(bf16[16,128]{1,0:T(8,128)(2,1)} %get-tuple-element.47) | copy-start | bytes 12292
  70.2 43.3 %collective-permute-start.7 = (bf16[5120,128]{1,0:T(8,128)(2,1)S(1)}, bf16[5120,128]{1,0:T(8,128)(2,1)}, u32[]{:S(2)}, u32[]{:S(2)}) collective-permute-start(bf16[5120,128]{1,0:T(8,128)(2,1)S(1)} %pad_maximum_fusion.1.refs_0_), channel_id=1, source_target_pairs={{0,32},{32,0},{64,96},{96,64},{1,33},{33,1},{65,97},{97,65},{2,34}... | collective-permute-start | bytes 3932168 | tf_op jit(solution)/shard_map/ppermute | solution.py:251
  72.8 43.6 %collective-permute-start.3 = (bf16[5120,128]{1,0:T(8,128)(2,1)S(1)}, bf16[5120,128]{1,0:T(8,128)(2,1)}, u32[]{:S(2)}, u32[]{:S(2)}) collective-permute-start(bf16[5120,128]{1,0:T(8,128)(2,1)S(1)} %pad_maximum_fusion.refs_0_), channel_id=1, source_target_pairs={{32,64},{64,32},{96,0},{0,96},{33,65},{65,33},{97,1},{1,97},{34,66... | collective-permute-start | bytes 3932168 | tf_op jit(solution)/shard_map/ppermute | solution.py:251
  78.1 43.0 %collective-permute-start.15 = (bf16[4480,128]{1,0:T(8,128)(2,1)}, bf16[4480,128]{1,0:T(8,128)(2,1)}, u32[]{:S(2)}, u32[]{:S(2)}) collective-permute-start(bf16[4480,128]{1,0:T(8,128)(2,1)} %pad_maximum_fusion.3.refs_2_), channel_id=1, source_target_pairs={{128,256},{256,128},{384,0},{0,384},{129,257},{257,129},{385,1},{1... | collective-permute-start | bytes 3440648 | tf_op jit(solution)/shard_map/ppermute | solution.py:251
